TPU v7x, 128 devices: a whole 4x4x4 slice. The times are simulated.
128 devices in a mesh: batch: 1, rows: 128 (over z, y, x, core).
Axes of the slice: x: 4, y: 4, z: 4, core: 2. Of those that a mesh axis runs over, the one named last changes fastest.
Arguments:
- a_mat: float32 [131072, 512], P(('batch', 'rows'))
- b_mat: float32 [131072, 512], P(('batch', 'rows'))
Outputs:
- output 1: float32 [131072, 512], P(('batch', 'rows'))
- output 2: float32 [512, 512], P('batch')
- output 3: float32 [131072, 512], P(('batch', 'rows'))
- output 4: float32 [512, 512], P('batch')
All inputs are finite; a program needn't handle non-finite values.
Results may differ from a plain program's by a relative error of at most 0.001.
Values sent between devices are 32-bit elements.
A program may use at most 1 GiB of HBM per device.

v0:
```python
import jax
import jax.numpy as jnp
from jax import lax
from jax.sharding import PartitionSpec as P

FULL_PRECISION = lax.Precision.HIGHEST


def gram_sweep(row_block, total_rows):
    local_gram = lax.dot_general(row_block, row_block, (((0,), (0,)), ((), ())), precision=FULL_PRECISION, preferred_element_type=jnp.float32)
    gram_sum = lax.psum(local_gram, "rows") / total_rows
    lower_fac = jnp.linalg.cholesky(gram_sum)
    ortho_rows = lax.linalg.triangular_solve(lower_fac, row_block, left_side=False, lower=True, transpose_a=True)
    return ortho_rows, lower_fac


def cholesky_qr2(row_block, total_rows):
    q_first, lower_first = gram_sweep(row_block, total_rows)
    q_final, lower_second = gram_sweep(q_first, total_rows)
    r_factor = lax.dot_general(lower_second, lower_first, (((0,), (1,)), ((), ())), precision=FULL_PRECISION, preferred_element_type=jnp.float32)
    return q_final, r_factor


def solution(mesh):
    group_size = mesh.shape["rows"]
    row_spec = P(("batch", "rows"), None)
    tri_spec = P("batch", None)

    def local_qr(block_a, block_b):
        total_rows = block_a.shape[0] * group_size
        a_ortho, a_upper = cholesky_qr2(block_a, total_rows)
        b_ortho, b_upper = cholesky_qr2(block_b, total_rows)
        return a_ortho, a_upper, b_ortho, b_upper

    return jax.shard_map(local_qr, mesh=mesh, in_specs=(row_spec, row_spec), out_specs=(row_spec, tri_spec, row_spec, tri_spec), check_vma=False)
```

profile of v0, /device:TPU:1, one launch (start us, length us, event | category | flops | bytes accessed | tf_op | source)
XLA Modules:
  0.0 985.6 jit_solution(1653693208896598824)
XLA Ops:
  7.2 6.8 fusion.188
  14.1 4.5 fusion.189
  18.9 155.5 %all-reduce.8.cloned.1.call-done = (f32[512,512]{0,1:T(8,128)}, f32[512,512]{0,1:T(8,128)}) async-done(((f32[512,512]{0,1:T(8,128)}, f32[512,512]{0,1:T(8,128)}), (f32[512,512]{0,1:T(8,128)}, f32[512,512]{0,1:T(8,128)})) %all-reduce.8.cloned.1.call-update) | async-done | bytes 2097168 | tf_op jit(solution)/shard_map/psum | solution.py:11
  179.7 3.6 fusion.65
  184.3 11.7 %cholesky.606 = f32[128,128]{1,0:T(8,128)S(1)} custom-call(f32[128,128]{1,0:T(8,128)S(1)} %cholesky.772), custom_call_target="Cholesky" | custom-call | tf_op jit(solution)/shard_map/jit(cholesky)/cholesky | solution.py:12
  196.0 9.8 custom-call.43
  208.5 11.7 %cholesky.625 = f32[128,128]{1,0:T(8,128)S(1)} custom-call(f32[128,128]{1,0:T(8,128)S(1)} %cholesky.776), custom_call_target="Cholesky" | custom-call | tf_op jit(solution)/shard_map/jit(cholesky)/cholesky | solution.py:12
  220.2 10.2 %custom-call.44 = f32[1,128,128]{1,2,0:T(8,128)S(1)} custom-call(f32[1,128,128]{2,1,0:T(8,128)S(1)} %get-tuple-element.110), custom_call_target="InvertDiagBlocksLowerTriangular" | custom-call | tf_op jit(solution)/shard_map/jit(cholesky)/cholesky | solution.py:12
  232.1 11.7 %cholesky.646 = f32[128,128]{1,0:T(8,128)S(1)} custom-call(f32[128,128]{1,0:T(8,128)S(1)} %cholesky.781), custom_call_target="Cholesky" | custom-call | tf_op jit(solution)/shard_map/jit(cholesky)/cholesky | solution.py:12
  245.8 9.8 custom-call.45
  257.0 11.9 %cholesky.663 = f32[128,128]{1,0:T(8,128)S(1)} custom-call(f32[128,128]{1,0:T(8,128)S(1)} %convolution_subtract_fusion.17), custom_call_target="Cholesky" | custom-call | tf_op jit(solution)/shard_map/jit(cholesky)/cholesky | solution.py:12
  274.1 14.1 %while.10 = (s32[]{:T(128)}, f32[512,512]{1,0:T(8,128)}, s32[4,2]{0,1:T(2,128)S(1)}, f32[4,128,128]{2,1,0:T(8,128)}, s32[]{:T(128)}) while((s32[]{:T(128)}, f32[512,512]{1,0:T(8,128)}, s32[4,2]{0,1:T(2,128)S(1)}, f32[4,128,128]{2,1,0:T(8,128)}, s32[]{:T(128)}) %tuple.101), condition=%wide.while_cond.clone.1, body=%wide.while_body.clone.1.sunk | while | flops 2 | bytes 132705 | solution.py:13
  274.7 2.9 bitcast_dynamic-update-slice_fusion.10
  288.2 40.7 %custom-call.46 = f32[4,128,128]{1,2,0:T(8,128)} custom-call(f32[4,128,128]{2,1,0:T(8,128)} %get-tuple-element.34), custom_call_target="InvertDiagBlocksLowerTriangular" | custom-call | tf_op jit(solution)/shard_map/triangular_solve/custom-call.3 | solution.py:13
  336.5 3.8 fusion.43
  341.0 4.5 fusion.8
  345.6 12.1 %cholesky.462 = f32[128,128]{1,0:T(8,128)S(1)} custom-call(f32[128,128]{1,0:T(8,128)S(1)} %cholesky.746), custom_call_target="Cholesky" | custom-call | tf_op jit(solution)/shard_map/jit(cholesky)/cholesky | solution.py:12
  357.7 9.8 custom-call.35
  370.0 11.7 %cholesky.481 = f32[128,128]{1,0:T(8,128)S(1)} custom-call(f32[128,128]{1,0:T(8,128)S(1)} %cholesky.750), custom_call_target="Cholesky" | custom-call | tf_op jit(solution)/shard_map/jit(cholesky)/cholesky | solution.py:12
  382.3 9.9 %custom-call.36 = f32[1,128,128]{1,2,0:T(8,128)S(1)} custom-call(f32[1,128,128]{2,1,0:T(8,128)S(1)} %get-tuple-element.120), custom_call_target="InvertDiagBlocksLowerTriangular" | custom-call | tf_op jit(solution)/shard_map/jit(cholesky)/cholesky | solution.py:12
  394.6 11.7 %cholesky.502 = f32[128,128]{1,0:T(8,128)S(1)} custom-call(f32[128,128]{1,0:T(8,128)S(1)} %cholesky.755), custom_call_target="Cholesky" | custom-call | tf_op jit(solution)/shard_map/jit(cholesky)/cholesky | solution.py:12
  409.0 9.8 custom-call.37
  421.1 11.7 %cholesky.519 = f32[128,128]{1,0:T(8,128)S(1)} custom-call(f32[128,128]{1,0:T(8,128)S(1)} %convolution_subtract_fusion.19), custom_call_target="Cholesky" | custom-call | tf_op jit(solution)/shard_map/jit(cholesky)/cholesky | solution.py:12
  439.0 12.0 %while.8 = (s32[]{:T(128)}, f32[512,512]{1,0:T(8,128)}, s32[4,2]{0,1:T(2,128)S(1)}, f32[4,128,128]{2,1,0:T(8,128)S(1)}, s32[]{:T(128)}) while((s32[]{:T(128)}, f32[512,512]{1,0:T(8,128)}, s32[4,2]{0,1:T(2,128)S(1)}, f32[4,128,128]{2,1,0:T(8,128)S(1)}, s32[]{:T(128)}) %tuple.116), condition=%wide.while_cond, body=%wide.while_body.sunk | while | flops 2 | bytes 131181 | solution.py:13
  451.0 40.3 %custom-call.38 = f32[4,128,128]{1,2,0:T(8,128)} custom-call(f32[4,128,128]{2,1,0:T(8,128)S(1)} %get-tuple-element.32), custom_call_target="InvertDiagBlocksLowerTriangular" | custom-call | tf_op jit(solution)/shard_map/triangular_solve/custom-call.3 | solution.py:13
  498.9 3.8 fusion.49
  504.3 4.5 fusion
  508.8 151.0 %all-reduce.6.cloned.1.call-done = (f32[512,512]{0,1:T(8,128)}, f32[512,512]{0,1:T(8,128)}) async-done(((f32[512,512]{0,1:T(8,128)}, f32[512,512]{0,1:T(8,128)}), (f32[512,512]{0,1:T(8,128)}, f32[512,512]{0,1:T(8,128)})) %all-reduce.6.cloned.1.call-update) | async-done | bytes 2097168 | tf_op jit(solution)/shard_map/psum | solution.py:11
  665.1 11.7 %cholesky.678 = f32[128,128]{1,0:T(8,128)S(1)} custom-call(f32[128,128]{1,0:T(8,128)S(1)} %cholesky.785), custom_call_target="Cholesky" | custom-call | tf_op jit(solution)/shard_map/jit(cholesky)/cholesky | solution.py:12
  677.0 9.8 custom-call.47
  689.4 11.7 %cholesky.697 = f32[128,128]{1,0:T(8,128)S(1)} custom-call(f32[128,128]{1,0:T(8,128)S(1)} %cholesky.789), custom_call_target="Cholesky" | custom-call | tf_op jit(solution)/shard_map/jit(cholesky)/cholesky | solution.py:12
  702.5 10.0 %custom-call.48 = f32[1,128,128]{1,2,0:T(8,128)S(1)} custom-call(f32[1,128,128]{2,1,0:T(8,128)S(1)} %get-tuple-element.90), custom_call_target="InvertDiagBlocksLowerTriangular" | custom-call | tf_op jit(solution)/shard_map/jit(cholesky)/cholesky | solution.py:12
  714.1 11.7 %cholesky.718 = f32[128,128]{1,0:T(8,128)S(1)} custom-call(f32[128,128]{1,0:T(8,128)S(1)} %cholesky.794), custom_call_target="Cholesky" | custom-call | tf_op jit(solution)/shard_map/jit(cholesky)/cholesky | solution.py:12
  726.4 9.8 custom-call.49
  737.7 11.7 %cholesky.735 = f32[128,128]{1,0:T(8,128)S(1)} custom-call(f32[128,128]{1,0:T(8,128)S(1)} %convolution_subtract_fusion.16), custom_call_target="Cholesky" | custom-call | tf_op jit(solution)/shard_map/jit(cholesky)/cholesky | solution.py:12
  752.7 3.7 fusion.77
  761.3 11.7 %cholesky.534 = f32[128,128]{1,0:T(8,128)S(1)} custom-call(f32[128,128]{1,0:T(8,128)S(1)} %cholesky.759), custom_call_target="Cholesky" | custom-call | tf_op jit(solution)/shard_map/jit(cholesky)/cholesky | solution.py:12
  773.2 9.8 custom-call.39
  785.5 11.9 %cholesky.553 = f32[128,128]{1,0:T(8,128)S(1)} custom-call(f32[128,128]{1,0:T(8,128)S(1)} %cholesky.763), custom_call_target="Cholesky" | custom-call | tf_op jit(solution)/shard_map/jit(cholesky)/cholesky | solution.py:12
  798.8 9.8 custom-call.40
  810.2 11.7 %cholesky.574 = f32[128,128]{1,0:T(8,128)S(1)} custom-call(f32[128,128]{1,0:T(8,128)S(1)} %cholesky.768), custom_call_target="Cholesky" | custom-call | tf_op jit(solution)/shard_map/jit(cholesky)/cholesky | solution.py:12
  822.6 9.8 custom-call.41
  833.8 11.9 %cholesky.591 = f32[128,128]{1,0:T(8,128)S(1)} custom-call(f32[128,128]{1,0:T(8,128)S(1)} %convolution_subtract_fusion.18), custom_call_target="Cholesky" | custom-call | tf_op jit(solution)/shard_map/jit(cholesky)/cholesky | solution.py:12
  848.9 4.5 fusion.74
  854.5 12.0 %while.11 = (s32[]{:T(128)}, f32[512,512]{1,0:T(8,128)}, s32[4,2]{0,1:T(2,128)S(1)}, f32[4,128,128]{2,1,0:T(8,128)S(1)}, s32[]{:T(128)}) while((s32[]{:T(128)}, f32[512,512]{1,0:T(8,128)}, s32[4,2]{0,1:T(2,128)S(1)}, f32[4,128,128]{2,1,0:T(8,128)S(1)}, s32[]{:T(128)}) %tuple.117), condition=%wide.while_cond.clone.2, body=%wide.while_body.clone.2.sunk | while | flops 2 | bytes 131181 | solution.py:13
  866.6 39.3 %custom-call.50 = f32[4,128,128]{1,2,0:T(8,128)S(1)} custom-call(f32[4,128,128]{2,1,0:T(8,128)S(1)} %get-tuple-element.35), custom_call_target="InvertDiagBlocksLowerTriangular" | custom-call | tf_op jit(solution)/shard_map/triangular_solve/custom-call.3 | solution.py:13
  917.6 11.7 %while.9 = (s32[]{:T(128)}, f32[512,512]{1,0:T(8,128)}, s32[4,2]{0,1:T(2,128)S(1)}, f32[4,128,128]{2,1,0:T(8,128)S(1)}, s32[]{:T(128)}) while((s32[]{:T(128)}, f32[512,512]{1,0:T(8,128)}, s32[4,2]{0,1:T(2,128)S(1)}, f32[4,128,128]{2,1,0:T(8,128)S(1)}, s32[]{:T(128)}) %tuple.118), condition=%wide.while_cond.clone, body=%wide.while_body.clone.sunk | while | flops 2 | bytes 131181 | solution.py:13
  929.3 39.3 %custom-call.42 = f32[4,128,128]{1,2,0:T(8,128)S(1)} custom-call(f32[4,128,128]{2,1,0:T(8,128)S(1)} %get-tuple-element.33), custom_call_target="InvertDiagBlocksLowerTriangular" | custom-call | tf_op jit(solution)/shard_map/triangular_solve/custom-call.3 | solution.py:13
  (227 shorter events, 144.0 us)
Async XLA Ops:
  7.2 6.9 copy-start
  7.2 167.2 %all-reduce.8.cloned.1.call-start = ((), (), s32[]{:S(2)}) async-start(), calls=%async_computation.1 | async-start | bytes 4194304 | tf_op jit(solution)/shard_map/psum | solution.py:11
  18.6 641.2 %all-reduce.6.cloned.1.call-start = ((), (), s32[]{:S(2)}) async-start(), calls=%async_computation | async-start | bytes 4194304 | tf_op jit(solution)/shard_map/psum | solution.py:11
  183.3 1.0 copy-start.18
  268.9 19.3 %copy-start.6 = (f32[512,512]{1,0:T(8,128)}, f32[512,512]{1,0:T(8,128)S(1)}, u32[]{:S(2)}) copy-start(f32[512,512]{1,0:T(8,128)S(1)} %get-tuple-element.105) | copy-start | bytes 3145732
  328.9 3.4 copy-start.25
  333.0 8.0 copy-start.2
  336.5 9.1 copy-start.8
  341.0 4.6 copy-start.19
  341.0 4.6 copy-start.17
  394.6 96.8 %copy-start.1 = (f32[1024,512]{1,0:T(8,128)S(1)}, f32[1024,512]{1,0:T(8,128)}, u32[]{:S(2)}) copy-start(f32[1024,512]{1,0:T(8,128)} %param.5) | copy-start | bytes 6291460
  491.4 3.4 copy-start.26
  495.4 8.0 copy-start.4
  498.9 4.5 copy-start.10
  503.4 0.8 copy-start.21
  659.8 3.9 copy-start.14
  664.1 1.0 copy-start.15
  677.0 75.6 %copy-start.7 = (f32[512,512]{1,0:T(8,128)S(1)}, f32[512,512]{1,0:T(8,128)}, u32[]{:S(2)}) copy-start(f32[512,512]{1,0:T(8,128)} %copy-done.6) | copy-start | bytes 3145732
  752.6 4.8 copy-start.12
  757.4 2.6 copy-start.13
  760.3 1.0 copy-start.16
  853.4 53.8 %copy-start.3 = (f32[1024,128]{0,1:T(8,128)S(1)}, f32[1024,128]{0,1:T(8,128)}, u32[]{:S(2)}) copy-start(f32[1024,128]{0,1:T(8,128)} %copy-done.2) | copy-start | bytes 1572868
  866.6 43.7 %copy-start.9 = (f32[1024,128]{0,1:T(8,128)S(1)}, f32[1024,128]{0,1:T(8,128)}, u32[]{:S(2)}) copy-start(f32[1024,128]{0,1:T(8,128)} %copy-done.8) | copy-start | bytes 1572868
  905.9 0.7 copy-start.23
  907.3 4.7 copy-start.24
  908.8 3.8 copy-start.20
  917.5 51.7 %copy-start.5 = (f32[1024,128]{0,1:T(8,128)S(1)}, f32[1024,128]{0,1:T(8,128)}, u32[]{:S(2)}) copy-start(f32[1024,128]{0,1:T(8,128)} %copy-done.4) | copy-start | bytes 1572868
  929.3 42.1 %copy-start.11 = (f32[1024,128]{0,1:T(8,128)S(1)}, f32[1024,128]{0,1:T(8,128)}, u32[]{:S(2)}) copy-start(f32[1024,128]{0,1:T(8,128)} %copy-done.10) | copy-start | bytes 1572868
  970.7 2.9 copy-start.22
Sparse Core Ops, SparseCore 0:
  18.7 155.6 all-reduce.7
  508.9 150.7 all-reduce.5
where the time goes:
time: 993 us; the launch traced here: 986 us
  other arithmetic  496 us (50%)
  waiting for transfers between devices  307 us (31%)
  matrix products  91 us (9%)
  local copies, waits for them, and re-layouts  66.1 us (7%)
  between operations  25.7 us (3%)
    another operation x60, other arithmetic, gram_sweep(): lower_fac = jnp.linalg.cholesky(gram_sum)  320 us
    psum x2, waiting for transfers between devices, gram_sweep(): gram_sum = lax.psum(local_gram, 'rows') / total_rows  306 us
    another operation x11, other arithmetic, gram_sweep(): lax.linalg.triangular_solve(lower_fac, row_block, left_side=False, lower=...  166 us
    another operation x53, local copies, waits for them, and re-layouts, gram_sweep(): lax.linalg.triangular_solve(lower_fac, row_block, left_side=False, lower=...  50.4 us
    another operation x28, matrix products, gram_sweep(): lax.linalg.triangular_solve(lower_fac, row_block, left_side=False, lower=...  40.2 us
    another operation x24, matrix products, gram_sweep(): lower_fac = jnp.linalg.cholesky(gram_sum)  22.3 us
    dot_general x4, matrix products, gram_sweep(): lax.dot_general(row_block, row_block, (((0,), (0,)), ((), ())), precision...  20.4 us
  transfers between devices with their start and end apart: 2, of which 2 were waited for; matrix products, arithmetic and copies ran while one was open for 0% of the time, Pallas kernels for 0%

commit v1 on v0

v1 whole, which is shorter than its diff:
```python
import functools

import jax
import jax.numpy as jnp
from jax import lax
from jax.experimental import pallas as pl
from jax.experimental.pallas import tpu as pltpu
from jax.sharding import PartitionSpec as P

FULL_PRECISION = lax.Precision.HIGHEST
F32 = jnp.float32
COLS = 512
ROWS = 1024
TILE = 128
BLOCKS = [(p, q) for p in range(4) for q in range(p, 4)]
PACKED = TILE * len(BLOCKS)
PART = PACKED // 4
PIECE = 24
PLANE = 16 * PIECE
VMEM = pl.BlockSpec(memory_space=pltpu.VMEM)
ANY = pl.BlockSpec(memory_space=pl.ANY)


def dot(a, b, ca, cb):
    return lax.dot_general(a, b, (((ca,), (cb,)), ((), ())), precision=FULL_PRECISION, preferred_element_type=F32)


def shape(*dims):
    return jax.ShapeDtypeStruct(dims, F32)


def row_of(x, k):
    return jnp.broadcast_to(x[k:k + 1, :], (8, TILE))


def col_of(x, k):
    return jnp.broadcast_to(x[:, k:k + 1], (8, TILE))


def factor_block(d_ref, w_ref):
    sub = lax.broadcasted_iota(jnp.int32, (8, TILE), 0)
    lane = lax.broadcasted_iota(jnp.int32, (8, TILE), 1)
    for kb in range(16):
        lo = 8 * kb
        rows = d_ref[lo:lo + 8, :]
        inv = w_ref[lo:lo + 8, :] + jnp.where(lane == sub + lo, 1.0, 0.0)
        cols = [col_of(rows, lo + j) for j in range(8)]
        scale, urow, wrow, low = [], [], [], {}
        for k in range(8):
            rs = lax.rsqrt(row_of(cols[k], k))
            lk = cols[k] * rs
            for j in range(k + 1, 8):
                low[j, k] = row_of(lk, j)
                cols[j] = cols[j] - lk * low[j, k]
            u, w = row_of(rows, k) * rs, row_of(inv, k) * rs
            lm = jnp.where(sub > k, lk, 0.0)
            rows = jnp.where(sub == k, u, rows - lm * u)
            inv = jnp.where(sub == k, w, inv - lm * w)
            scale.append(rs)
            urow.append(u)
            wrow.append(w)
        d_ref[lo:lo + 8, :] = jnp.where(lane >= sub + lo, rows, 0.0)
        w_ref[lo:lo + 8, :] = inv
        for m in range(kb + 1, 16):
            r = d_ref[8 * m:8 * m + 8, :]
            v = w_ref[8 * m:8 * m + 8, :]
            cs = [col_of(r, lo + j) for j in range(8)]
            for k in range(8):
                lk = cs[k] * scale[k]
                for j in range(k + 1, 8):
                    cs[j] = cs[j] - lk * low[j, k]
                r = r - lk * urow[k]
                v = v - lk * wrow[k]
            d_ref[8 * m:8 * m + 8, :] = r
            w_ref[8 * m:8 * m + 8, :] = v


def chol_kernel(g_ref, u_ref, m_ref, s_ref, d_ref, w_ref):
    s_ref[...] = jnp.zeros_like(s_ref)
    for i, (p, q) in enumerate(BLOCKS):
        s_ref[p, :, TILE * q:TILE * q + TILE] = g_ref[TILE * i:TILE * i + TILE, :]
    d_ref[...] = g_ref[0:TILE, :]

    def panel(p, carry):
        w_ref[...] = jnp.zeros_like(w_ref)
        factor_block(d_ref, w_ref)
        for pp in range(4):
            @pl.when(p == pp)
            def _():
                lo, hi = TILE * pp, TILE * pp + TILE
                w = w_ref[...]
                u_ref[lo:hi, :] = jnp.zeros((TILE, COLS), F32)
                m_ref[lo:hi, :] = jnp.zeros((TILE, COLS), F32)
                u_ref[lo:hi, lo:hi] = d_ref[...]
                m_ref[lo:hi, lo:hi] = w
                if pp > 0:
                    m_ref[lo:hi, 0:lo] = dot(w, s_ref[pp, :, 0:lo], 1, 0)
                if pp < 3:
                    right = dot(w, s_ref[pp, :, hi:], 1, 0)
                    u_ref[lo:hi, hi:] = right
                    for q in range(pp + 1, 4):
                        off = TILE * (q - pp - 1)
                        piece = right[:, off:off + TILE]
                        new = s_ref[q, :, TILE * q:] - dot(piece, right[:, off:], 0, 0)
                        s_ref[q, :, TILE * q:] = new
                        if q == pp + 1:
                            d_ref[...] = new[:, 0:TILE]
                        s_ref[q, :, 0:hi] = s_ref[q, :, 0:hi] - dot(piece, m_ref[lo:hi, 0:hi], 0, 0)
        return carry

    lax.fori_loop(0, 4, panel, 0)


def chol(gram):
    return pl.pallas_call(
        chol_kernel,
        name="chol",
        out_shape=[shape(COLS, COLS)] * 2,
        in_specs=[VMEM],
        out_specs=[VMEM, VMEM],
        scratch_shapes=[pltpu.VMEM((4, TILE, COLS), F32), pltpu.VMEM((TILE, TILE), F32), pltpu.VMEM((TILE, TILE), F32)],
    )(gram)


class Place:
    def __init__(self):
        self.me = lax.axis_index("rows")
        core = lax.rem(self.me, 2)
        x, y, z = (lax.rem(self.me // s, 4) for s in (2, 8, 32))
        self.core = core
        self.steps = (2 + 6 * core, 8 + 24 * core, 32 - 30 * core)
        self.spots = tuple(a + core * (b - a) for a, b in ((x, y), (y, z), (z, x)))
        self.partner = self.me + 1 - 2 * core

    def shifted(self, dim, j):
        spot = lax.rem(self.spots[dim] + j, 4)
        return spot, (spot - self.spots[dim]) * self.steps[dim]


PLANE_HOPS = [(j, k) for j in range(4) for k in range(4) if (j, k) != (0, 0)]


def remote(src, dst, send, recv, device):
    return pltpu.make_async_remote_copy(src_ref=src, dst_ref=dst, send_sem=send, recv_sem=recv, device_id={"rows": device}, device_id_type=pl.DeviceIdType.MESH)


def greet(place):
    barrier = pltpu.get_barrier_semaphore()
    peers = [place.partner]
    peers += [place.me + place.shifted(0, j)[1] for j in range(1, 4)]
    peers += [place.me + place.shifted(1, j)[1] + place.shifted(2, k)[1] for j, k in PLANE_HOPS]
    for peer in peers:
        pl.semaphore_signal(barrier, inc=1, device_id={"rows": peer}, device_id_type=pl.DeviceIdType.MESH)
    return lambda: pl.semaphore_wait(barrier, len(peers))


def sum_scratch():
    return [
        pltpu.VMEM((3, PART, TILE), F32),
        pltpu.VMEM((PLANE, TILE), F32),
        pltpu.VMEM((15, PIECE, TILE), F32),
        pltpu.VMEM((PLANE, TILE), F32),
        pltpu.VMEM((PACKED, TILE), F32),
        pltpu.SemaphoreType.DMA((2, 36)),
    ]


def ds(i, size):
    return pl.ds(pl.multiple_of(i * size, 8), size)


def all_sum(place, g_ref, got1, acc, got2, full, out, sems, inv_rows):
    copies = []

    def send(src, dst, device):
        copy = remote(src, dst, sems.at[0, len(copies)], sems.at[1, len(copies)], device)
        copy.start()
        copies.append(copy)
        return copy

    first = []
    for j in range(1, 4):
        spot, step = place.shifted(0, j)
        first.append(send(g_ref.at[ds(spot, PART)], got1.at[j - 1], place.me + step))
    acc[PART:, :] = jnp.zeros((PLANE - PART, TILE), F32)
    for copy in first:
        copy.wait_recv()
    acc[0:PART, :] = (g_ref[ds(place.spots[0], PART), :] + got1[0]) + (got1[1] + got1[2])
    second = []
    for i, (j, k) in enumerate(PLANE_HOPS):
        (spot1, step1), (spot2, step2) = place.shifted(1, j), place.shifted(2, k)
        second.append(send(acc.at[ds(spot1 * 4 + spot2, PIECE)], got2.at[i], place.me + step1 + step2))
    mine = place.spots[1] * 4 + place.spots[2]
    total = acc[ds(mine, PIECE), :]
    for i, copy in enumerate(second):
        copy.wait_recv()
        total = total + got2[i]
    full[ds(mine, PIECE), :] = total * inv_rows
    third = []
    for i, (j, k) in enumerate(PLANE_HOPS):
        step1, step2 = place.shifted(1, j)[1], place.shifted(2, k)[1]
        spot = full.at[ds(mine, PIECE)]
        third.append(send(spot, spot, place.me + step1 + step2))
    for copy in third:
        copy.wait_recv()
    last = []
    here = ds(place.spots[0], PART)
    for j in range(1, 4):
        last.append(send(full.at[0:PART], out.at[here], place.me + place.shifted(0, j)[1]))
    out[here, :] = full[0:PART, :]
    for copy in last:
        copy.wait_recv()
    for copy in copies:
        copy.wait_send()


def gram_into(x, dst):
    top = dot(x[:, 0:256], x[...], 0, 0)
    low = dot(x[:, 256:512], x[:, 256:512], 0, 0)
    for i, (p, q) in enumerate(BLOCKS):
        src, off = (top, 0) if p < 2 else (low, 256)
        dst[TILE * i:TILE * i + TILE, :] = src[TILE * p - off:TILE * p - off + TILE, TILE * q - off:TILE * q - off + TILE]


def first_kernel(inv_rows, a_ref, b_ref, out_ref, rows_ref, x, g, gx, local, swap, *scratch):
    place = Place()
    greeted = greet(place)
    for c, (other, own) in enumerate(((b_ref, a_ref), (a_ref, b_ref))):
        @pl.when(place.core == c)
        def _():
            pltpu.make_async_copy(other, x.at[0], local.at[0]).start()
            pltpu.make_async_copy(own, x.at[1], local.at[1]).start()
    pltpu.make_async_copy(a_ref, x.at[0], local.at[0]).wait()
    gram_into(x.at[0], g.at[0])
    greeted()
    give = remote(g.at[0], gx, swap.at[0], swap.at[1], place.partner)
    give.start()
    pltpu.make_async_copy(a_ref, x.at[1], local.at[1]).wait()
    gram_into(x.at[1], g.at[1])
    give.wait_recv()
    swap_rows = remote(x.at[0], rows_ref, swap.at[2], swap.at[3], place.partner)
    swap_rows.start()
    g[1] = g[1] + gx[...]
    *work, out, sems = scratch
    all_sum(place, g.at[1], *work, out, sems, inv_rows)
    out_ref[...] = out[...]
    give.wait_send()
    swap_rows.wait()


def first_sum(a, b, inv_rows):
    return pl.pallas_call(
        functools.partial(first_kernel, inv_rows),
        name="first_sum",
        out_shape=[shape(PACKED, TILE), shape(ROWS, COLS)],
        in_specs=[ANY, ANY],
        out_specs=[VMEM, ANY],
        scratch_shapes=[
            pltpu.VMEM((2, ROWS, COLS), F32),
            pltpu.VMEM((2, PACKED, TILE), F32),
            pltpu.VMEM((PACKED, TILE), F32),
            pltpu.SemaphoreType.DMA((2,)),
            pltpu.SemaphoreType.DMA((4,)),
            *sum_scratch(),
        ],
        compiler_params=pltpu.CompilerParams(collective_id=0, has_side_effects=True),
    )(a, b)


def solve_into(x, m, dst):
    dst[:, 0:256] = dot(x[:, 0:256], m[0:256, 0:256], 1, 1)
    dst[:, 256:512] = dot(x[...], m[256:512, :], 1, 1)


def second_kernel(inv_rows, a_ref, b_ref, rows_ref, m_ref, out_ref, own_ref, other_ref, x, q, g, local, swap, *scratch):
    place = Place()
    greeted = greet(place)
    for c, own in enumerate((a_ref, b_ref)):
        @pl.when(place.core == c)
        def _():
            pltpu.make_async_copy(own, x.at[1], local.at[1]).start()
    fetch = pltpu.make_async_copy(rows_ref, x.at[0], local.at[0])
    fetch.start()
    fetch.wait()
    solve_into(x.at[0], m_ref, q.at[0])
    greeted()
    swap_rows = remote(q.at[0], other_ref, swap.at[0], swap.at[1], place.partner)
    swap_rows.start()
    pltpu.make_async_copy(a_ref, x.at[1], local.at[1]).wait()
    solve_into(x.at[1], m_ref, q.at[1])
    keep = pltpu.make_async_copy(q.at[1], own_ref, local.at[2])
    keep.start()
    gram_into(q.at[0], g.at[0])
    gram_into(q.at[1], g.at[1])
    g[0] = g[0] + g[1]
    *work, out, sems = scratch
    all_sum(place, g.at[0], *work, out, sems, inv_rows)
    out_ref[...] = out[...]
    swap_rows.wait()
    keep.wait()


def second_sum(a, b, rows, m, inv_rows):
    return pl.pallas_call(
        functools.partial(second_kernel, inv_rows),
        name="second_sum",
        out_shape=[shape(PACKED, TILE), shape(ROWS, COLS), shape(ROWS, COLS)],
        in_specs=[ANY, ANY, ANY, VMEM],
        out_specs=[VMEM, ANY, ANY],
        scratch_shapes=[
            pltpu.VMEM((2, ROWS, COLS), F32),
            pltpu.VMEM((2, ROWS, COLS), F32),
            pltpu.VMEM((2, PACKED, TILE), F32),
            pltpu.SemaphoreType.DMA((3,)),
            pltpu.SemaphoreType.DMA((2,)),
            *sum_scratch(),
        ],
        compiler_params=pltpu.CompilerParams(collective_id=1, has_side_effects=True),
    )(a, b, rows, m)


def share_kernel(u1_ref, u2_ref, m_ref, ma_ref, mb_ref, ra_ref, rb_ref, r, got, sems):
    place = Place()
    barrier = pltpu.get_barrier_semaphore()
    pl.semaphore_signal(barrier, inc=1, device_id={"rows": place.partner}, device_id_type=pl.DeviceIdType.MESH)
    pl.semaphore_wait(barrier, 1)
    inv = remote(m_ref, got.at[0], sems.at[0], sems.at[1], place.partner)
    inv.start()
    r[...] = jnp.zeros_like(r)
    r[0:256, :] = dot(u2_ref[0:256, :], u1_ref[...], 1, 0)
    r[256:512, 256:512] = dot(u2_ref[256:512, 256:512], u1_ref[256:512, 256:512], 1, 0)
    tri = remote(r, got.at[1], sems.at[2], sems.at[3], place.partner)
    tri.start()
    inv.wait_recv()
    tri.wait_recv()
    for c, (m_own, m_other, r_own, r_other) in enumerate(((ma_ref, mb_ref, ra_ref, rb_ref), (mb_ref, ma_ref, rb_ref, ra_ref))):
        @pl.when(place.core == c)
        def _():
            m_own[...] = m_ref[...]
            r_own[...] = r[...]
            m_other[...] = got[0]
            r_other[...] = got[1]
    inv.wait_send()
    tri.wait_send()


def share(u1, u2, m):
    return pl.pallas_call(
        share_kernel,
        name="share",
        out_shape=[shape(COLS, COLS)] * 4,
        in_specs=[VMEM] * 3,
        out_specs=[VMEM] * 4,
        scratch_shapes=[pltpu.VMEM((COLS, COLS), F32), pltpu.VMEM((2, COLS, COLS), F32), pltpu.SemaphoreType.DMA((4,))],
        compiler_params=pltpu.CompilerParams(collective_id=2, has_side_effects=True),
    )(u1, u2, m)


def last_kernel(own_ref, other_ref, ma_ref, mb_ref, qa_ref, qb_ref):
    core = lax.rem(lax.axis_index("rows"), 2)
    for c, (qa, qb) in enumerate(((own_ref, other_ref), (other_ref, own_ref))):
        @pl.when(core == c)
        def _():
            solve_into(qa, ma_ref, qa_ref)
            solve_into(qb, mb_ref, qb_ref)


def last_solve(own, other, ma, mb):
    step = 256
    rows = pl.BlockSpec((step, COLS), lambda i: (i, 0))
    whole = pl.BlockSpec((COLS, COLS), lambda i: (0, 0))
    return pl.pallas_call(
        last_kernel,
        name="last_solve",
        grid=(ROWS // step,),
        out_shape=[shape(ROWS, COLS)] * 2,
        in_specs=[rows, rows, whole, whole],
        out_specs=[rows, rows],
    )(own, other, ma, mb)


def solution(mesh):
    row_spec = P(("batch", "rows"), None)
    tri_spec = P("batch", None)
    inv_rows = 1.0 / (ROWS * mesh.shape["rows"])

    def local_qr(a, b):
        gram1, rows = first_sum(a, b, inv_rows)
        u1, m1 = chol(gram1)
        gram2, own, other = second_sum(a, b, rows, m1, inv_rows)
        u2, m2 = chol(gram2)
        ma, mb, ra, rb = share(u1, u2, m2)
        qa, qb = last_solve(own, other, ma, mb)
        return qa, ra, qb, rb

    return jax.shard_map(local_qr, mesh=mesh, in_specs=(row_spec, row_spec), out_specs=(row_spec, tri_spec, row_spec, tri_spec), check_vma=False)
```

time: 993 us -> 146 us (0.15)
  other arithmetic: 496 us -> 0 us
  waiting for transfers between devices: 307 us -> 0 us
  Pallas kernels: 0 us -> 142 us
  matrix products: 91 us -> 0 us
  local copies, waits for them, and re-layouts: 66.1 us -> 2.57 us
  between operations: 25.7 us -> 0.67 us
    another operation x71 -> x0, other arithmetic: 485 us -> none  [the longest x60 320 us: gram_sweep(): lower_fac = jnp.linalg.cholesky(gram_sum)]
    psum x2 -> x0, waiting for transfers between devices: 306 us -> none  [gram_sweep(): gram_sum = lax.psum(local_gram, 'rows') / total_rows]
    pallas_call x0 -> x6, Pallas kernels: none -> 142 us  [the longest x1 41.3 us: second_sum(): pl.pallas_call(functools.partial(second_kernel, inv_rows), name='second_s...]
    another operation x52 -> x0, matrix products: 62.4 us -> none  [the longest x28 40.2 us: gram_sweep(): lax.linalg.triangular_solve(lower_fac, row_block, left_side=False, lower=...]
    another operation x69 -> x0, local copies, waits for them, and re-layouts: 52 us -> none  [the longest x53 50.4 us: gram_sweep(): lax.linalg.triangular_solve(lower_fac, row_block, left_side=False, lower=...]
    dot_general x6 -> x0, matrix products: 28.6 us -> none  [the longest x4 20.4 us: gram_sweep(): lax.dot_general(row_block, row_block, (((0,), (0,)), ((), ())), precision...]
    div x7 -> x0, other arithmetic: 10.3 us -> none  [the longest x4 6.08 us: gram_sweep(): gram_sum = lax.psum(local_gram, 'rows') / total_rows]
  transfers between devices with their start and end apart: 2 -> 0, of which waited for: 2 -> 0; matrix products, arithmetic and copies ran while one was open for 0% -> 0% of each run, Pallas kernels for 0% -> 0%
where the time goes in v1:
time: 146 us
  Pallas kernels  142 us (97%)
  local copies, waits for them, and re-layouts  2.57 us (2%)
    pallas_call x1, Pallas kernels, second_sum(): pl.pallas_call(functools.partial(second_kernel, inv_rows), name='second_s...  41.3 us
    pallas_call x2, Pallas kernels, chol(): pl.pallas_call(chol_kernel, name='chol', out_shape=[shape(COLS, COLS)] *...  40.3 us
    pallas_call x1, Pallas kernels, first_sum(): pl.pallas_call(functools.partial(first_kernel, inv_rows), name='first_sum...  36.7 us
    pallas_call x1, Pallas kernels, share(): pl.pallas_call(share_kernel, name='share', out_shape=[shape(COLS, COLS)]...  14.6 us
    pallas_call x1, Pallas kernels, last_solve(): pl.pallas_call(last_kernel, name='last_solve', grid=(ROWS // step,), out_...  9.42 us

profile of v1, /device:TPU:1, one launch (start us, length us, event | category | flops | bytes accessed | tf_op | source)
XLA Modules:
  0.0 145.6 jit_solution(1398330404070479617)
XLA Ops:
  0.6 36.7 %first_sum.1 = (f32[1280,128]{1,0:T(8,128)}, f32[1024,512]{1,0:T(8,128)}) custom-call(f32[1024,512]{1,0:T(8,128)} %a_ref.3, f32[1024,512]{1,0:T(8,128)} %b_ref.3), custom_call_target="tpu_custom_call" | custom-call | tf_op jit(solution)/shard_map/first_sum/pallas_call | solution.py:252
  37.3 20.3 %chol.2 = (f32[512,512]{1,0:T(8,128)}, f32[512,512]{1,0:T(8,128)}) custom-call(f32[1280,128]{1,0:T(8,128)} %get-tuple-element.20.g_ref), custom_call_target="tpu_custom_call" | custom-call | tf_op jit(solution)/shard_map/chol/pallas_call | solution.py:115
  57.6 41.3 %second_sum.1 = (f32[1280,128]{1,0:T(8,128)}, f32[1024,512]{1,0:T(8,128)}, f32[1024,512]{1,0:T(8,128)}) custom-call(f32[1024,512]{1,0:T(8,128)} %a_ref.3, f32[1024,512]{1,0:T(8,128)} %b_ref.3, f32[1024,512]{1,0:T(8,128)} %get-tuple-element.19.rows_ref, f32[512,512]{1,0:T(8,128)} %get-tuple-element.21.m_ref), custom_call_target="tpu_custom_call" | custom-call | tf_op jit(solution)/shard_map/second_sum/pallas_call | solution.py:304
  98.9 20.1 %chol.3 = (f32[512,512]{1,0:T(8,128)}, f32[512,512]{1,0:T(8,128)}) custom-call(f32[1280,128]{1,0:T(8,128)} %get-tuple-element.25.g_ref), custom_call_target="tpu_custom_call" | custom-call | tf_op jit(solution)/shard_map/chol/pallas_call | solution.py:115
  119.0 14.6 %share.1 = (f32[512,512]{1,0:T(8,128)}, f32[512,512]{1,0:T(8,128)}, f32[512,512]{1,0:T(8,128)}, f32[512,512]{1,0:T(8,128)}) custom-call(f32[512,512]{1,0:T(8,128)} %get-tuple-element.24.u1_ref, f32[512,512]{1,0:T(8,128)} %get-tuple-element.26.u2_ref, f32[512,512]{1,0:T(8,128)} %get-tuple-element.27.m_ref), custom_call_target="tpu_custom_call" | custom-call | tf_op jit(solution)/shard_map/share/pallas_call | solution.py:348
  133.6 0.0 copy-start.1
  133.6 9.4 %last_solve.1 = (f32[1024,512]{1,0:T(8,128)}, f32[1024,512]{1,0:T(8,128)}) custom-call(f32[1024,512]{1,0:T(8,128)} %get-tuple-element.22.own_ref, f32[1024,512]{1,0:T(8,128)} %get-tuple-element.23.other_ref, f32[512,512]{1,0:T(8,128)} %get-tuple-element.28.ma_ref, f32[512,512]{1,0:T(8,128)} %get-tuple-element.29.mb_ref), custom_call_target="tpu_custom_call" | custom-call | tf_op jit(solution)/shard_map/last_solve/pallas_call | solution.py:372
  143.0 0.0 copy-start
  143.0 0.0 copy-done.1
  143.0 1.0 copy.8
  144.0 0.6 copy-done
  144.6 1.0 copy.9
Async XLA Ops:
  133.6 9.4 %copy-start.1 = (f32[512,512]{1,0:T(8,128)S(1)}, f32[512,512]{1,0:T(8,128)}, u32[]{:S(2)}) copy-start(f32[512,512]{1,0:T(8,128)} %get-tuple-element.39) | copy-start | bytes 3145732
  143.0 1.6 %copy-start = (f32[512,512]{1,0:T(8,128)S(1)}, f32[512,512]{1,0:T(8,128)}, u32[]{:S(2)}) copy-start(f32[512,512]{1,0:T(8,128)} %get-tuple-element.41) | copy-start | bytes 3145732

commit v2 on v1

v2 whole, which is shorter than its diff:
```python
import functools

import jax
import jax.numpy as jnp
from jax import lax
from jax.experimental import pallas as pl
from jax.experimental.pallas import tpu as pltpu
from jax.sharding import PartitionSpec as P

FULL_PRECISION = lax.Precision.HIGHEST
F32 = jnp.float32
COLS = 512
ROWS = 1024
TILE = 128
BLOCKS = [(p, q) for p in range(4) for q in range(p, 4)]
PACKED = TILE * len(BLOCKS)
FIRST = 112
PART = 4 * FIRST
PADDED = 3 * PART
PIECE = 8
PLANE = 16 * PIECE
CHUNK = 512
H = COLS // 2
MIB = 1 << 20
VMEM = pl.BlockSpec(memory_space=pltpu.VMEM)
HBM = pl.BlockSpec(memory_space=pltpu.HBM)


def dot(a, b, ca, cb):
    return lax.dot_general(a, b, (((ca,), (cb,)), ((), ())), precision=FULL_PRECISION, preferred_element_type=F32)


def shape(*dims):
    return jax.ShapeDtypeStruct(dims, F32)


def row_of(x, k):
    return jnp.broadcast_to(x[k:k + 1, :], (8, TILE))


def col_of(x, k):
    return jnp.broadcast_to(x[:, k:k + 1], (8, TILE))


def factor_block(d_ref, w_ref):
    sub = lax.broadcasted_iota(jnp.int32, (8, TILE), 0)
    lane = lax.broadcasted_iota(jnp.int32, (8, TILE), 1)
    for kb in range(16):
        lo = 8 * kb
        rows = d_ref[lo:lo + 8, :]
        inv = w_ref[lo:lo + 8, :] + jnp.where(lane == sub + lo, 1.0, 0.0)
        cols = [col_of(rows, lo + j) for j in range(8)]
        scale, urow, wrow, low = [], [], [], {}
        for k in range(8):
            rs = lax.rsqrt(row_of(cols[k], k))
            lk = cols[k] * rs
            for j in range(k + 1, 8):
                low[j, k] = row_of(lk, j)
                cols[j] = cols[j] - lk * low[j, k]
            u, w = row_of(rows, k) * rs, row_of(inv, k) * rs
            lm = jnp.where(sub > k, lk, 0.0)
            rows = jnp.where(sub == k, u, rows - lm * u)
            inv = jnp.where(sub == k, w, inv - lm * w)
            scale.append(rs)
            urow.append(u)
            wrow.append(w)
        d_ref[lo:lo + 8, :] = jnp.where(lane >= sub + lo, rows, 0.0)
        w_ref[lo:lo + 8, :] = inv
        for m in range(kb + 1, 16):
            r = d_ref[8 * m:8 * m + 8, :]
            v = w_ref[8 * m:8 * m + 8, :]
            cs = [col_of(r, lo + j) for j in range(8)]
            for k in range(8):
                lk = cs[k] * scale[k]
                for j in range(k + 1, 8):
                    cs[j] = cs[j] - lk * low[j, k]
                r = r - lk * urow[k]
                v = v - lk * wrow[k]
            d_ref[8 * m:8 * m + 8, :] = r
            w_ref[8 * m:8 * m + 8, :] = v


def factor_all(g_ref, u_ref, m_ref, s_ref, d_ref, w_ref):
    s_ref[...] = jnp.zeros_like(s_ref)
    for i, (p, q) in enumerate(BLOCKS):
        s_ref[TILE * p:TILE * p + TILE, TILE * q:TILE * q + TILE] = g_ref[TILE * i:TILE * i + TILE, :]
    d_ref[...] = g_ref[0:TILE, :]

    def panel(p, carry):
        w_ref[...] = jnp.zeros_like(w_ref)
        factor_block(d_ref, w_ref)
        for pp in range(4):
            @pl.when(p == pp)
            def _():
                lo, hi = TILE * pp, TILE * pp + TILE
                w = w_ref[...]
                u_ref[lo:hi, :] = jnp.zeros((TILE, COLS), F32)
                m_ref[lo:hi, :] = jnp.zeros((TILE, COLS), F32)
                u_ref[lo:hi, lo:hi] = d_ref[...]
                m_ref[lo:hi, lo:hi] = w
                if pp > 0:
                    m_ref[lo:hi, 0:lo] = dot(w, s_ref[lo:hi, 0:lo], 1, 0)
                if pp < 3:
                    right = dot(w, s_ref[lo:hi, hi:], 1, 0)
                    u_ref[lo:hi, hi:] = right
                    for q in range(pp + 1, 4):
                        off, band = TILE * (q - pp - 1), slice(TILE * q, TILE * q + TILE)
                        piece = right[:, off:off + TILE]
                        new = s_ref[band, TILE * q:] - dot(piece, right[:, off:], 0, 0)
                        s_ref[band, TILE * q:] = new
                        if q == pp + 1:
                            d_ref[...] = new[:, 0:TILE]
                        s_ref[band, 0:hi] = s_ref[band, 0:hi] - dot(piece, m_ref[lo:hi, 0:hi], 0, 0)
        return carry

    lax.fori_loop(0, 4, panel, 0)


def chol(gram):
    return pl.pallas_call(
        factor_all,
        name="chol",
        out_shape=[shape(COLS, COLS)] * 2,
        in_specs=[VMEM],
        out_specs=[VMEM, VMEM],
        scratch_shapes=[pltpu.VMEM((COLS, COLS), F32), pltpu.VMEM((TILE, TILE), F32), pltpu.VMEM((TILE, TILE), F32)],
        compiler_params=pltpu.CompilerParams(vmem_limit_bytes=MIB * 12),
        cost_estimate=pl.CostEstimate(flops=10**10, bytes_accessed=3 * MIB, transcendentals=COLS),
    )(gram)


def lower_half(x, edge):
    if not edge:
        return x
    row = lax.broadcasted_iota(jnp.int32, x.shape, 0)
    col = lax.broadcasted_iota(jnp.int32, x.shape, 1)
    return jnp.where(row > col, x, jnp.where(row == col, 0.5 * x, 0.0))


def near_identity_step(e_ref, n_ref):
    n00, n10, n11 = n_ref[0:H, 0:H], n_ref[H:, 0:H], n_ref[H:, H:]
    e00, e10, e11 = e_ref[0:H, 0:H], e_ref[H:, 0:H], e_ref[H:, H:]
    e01 = e_ref[0:H, H:]
    p00 = dot(n00, e00, 1, 0)
    p1 = dot(n_ref[H:, :], e_ref[...], 1, 0)
    p10, p11 = p1[:, 0:H], p1[:, H:]
    s00 = e00 + n00 + n00.T + p00 + dot(e00 + n00 + p00, n00, 1, 1)
    s10 = e10 + n10 + p10 + dot(e10 + n10 + p10, n00, 1, 1)
    s11 = e11 + n11 + n11.T + p11 + dot(e_ref[H:, :] + n_ref[H:, :] + p1, n_ref[H:, :], 1, 1)
    size = jnp.sum(s00 * s00) + 2 * jnp.sum(s10 * s10) + jnp.sum(s11 * s11)
    s00, s11 = lower_half(s00, True), lower_half(s11, True)
    n_ref[0:H, 0:H] = n00 - (s00 + dot(s00, n00, 1, 0))
    n_ref[H:, 0:H] = n10 - (s10 + dot(s10, n00, 1, 0) + dot(s11, n10, 1, 0))
    n_ref[H:, H:] = n11 - (s11 + dot(s11, n11, 1, 0))
    return size


def refine_kernel(g_ref, u1_ref, m_ref, r_ref, e_ref, n_ref, d_ref, w_ref):
    row = lax.broadcasted_iota(jnp.int32, (TILE, TILE), 0)
    col = lax.broadcasted_iota(jnp.int32, (TILE, TILE), 1)
    size = jnp.zeros((), F32)
    for i, (p, q) in enumerate(BLOCKS):
        x = g_ref[TILE * i:TILE * i + TILE, :]
        if p == q:
            x = x - jnp.where(row == col, 1.0, 0.0)
            n_ref[TILE * p:TILE * p + TILE, TILE * p:TILE * p + TILE] = -lower_half(x, True)
        else:
            t = x.T
            e_ref[TILE * q:TILE * q + TILE, TILE * p:TILE * p + TILE] = t
            n_ref[TILE * q:TILE * q + TILE, TILE * p:TILE * p + TILE] = -t
            n_ref[TILE * p:TILE * p + TILE, TILE * q:TILE * q + TILE] = jnp.zeros((TILE, TILE), F32)
        e_ref[TILE * p:TILE * p + TILE, TILE * q:TILE * q + TILE] = x
        size = size + (1 if p == q else 2) * jnp.sum(x * x)
    near = size < 0.1

    @pl.when(near)
    def _():
        lax.while_loop(lambda s: s > 1e-7, lambda s: near_identity_step(e_ref, n_ref), jnp.ones((), F32))
        n00, n1 = n_ref[0:H, 0:H], n_ref[H:, :]
        p0 = dot(n00, e_ref[0:H, :], 1, 0)
        p11 = dot(n1, e_ref[:, H:], 1, 0)
        f00 = e_ref[0:H, 0:H] + n00 + p0[:, 0:H]
        f01 = e_ref[0:H, H:] + p0[:, H:]
        f11 = e_ref[H:, H:] + n1[:, H:] + p11
        r2 = lax.broadcasted_iota(jnp.int32, (H, H), 0)
        c2 = lax.broadcasted_iota(jnp.int32, (H, H), 1)
        f00, f11 = jnp.where(r2 <= c2, f00, 0.0), jnp.where(r2 <= c2, f11, 0.0)
        r_ref[0:H, 0:H] = u1_ref[0:H, 0:H] + dot(f00, u1_ref[0:H, 0:H], 1, 0)
        r_ref[0:H, H:] = u1_ref[0:H, H:] + (dot(f00, u1_ref[0:H, H:], 1, 0) + dot(f01, u1_ref[H:, H:], 1, 0))
        r_ref[H:, 0:H] = jnp.zeros((H, H), F32)
        r_ref[H:, H:] = u1_ref[H:, H:] + dot(f11, u1_ref[H:, H:], 1, 0)
        for p in range(4):
            for q in range(4):
                x = n_ref[TILE * p:TILE * p + TILE, TILE * q:TILE * q + TILE]
                if p == q:
                    x = x + jnp.where(row == col, 1.0, 0.0)
                m_ref[TILE * p:TILE * p + TILE, TILE * q:TILE * q + TILE] = x

    @pl.when(jnp.logical_not(near))
    def _():
        factor_all(g_ref, e_ref, m_ref, n_ref, d_ref, w_ref)
        r_ref[0:H, :] = dot(e_ref[0:H, :], u1_ref[...], 1, 0)
        r_ref[H:, 0:H] = jnp.zeros((H, H), F32)
        r_ref[H:, H:] = dot(e_ref[H:, H:], u1_ref[H:, H:], 1, 0)

def refine(gram, u1):
    return pl.pallas_call(
        refine_kernel,
        name="refine",
        out_shape=[shape(COLS, COLS)] * 2,
        in_specs=[VMEM, VMEM],
        out_specs=[VMEM, VMEM],
        scratch_shapes=[pltpu.VMEM((COLS, COLS), F32)] * 2 + [pltpu.VMEM((TILE, TILE), F32)] * 2,
        compiler_params=pltpu.CompilerParams(vmem_limit_bytes=MIB * 16),
    )(gram, u1)


STEPS = (2, 8, 32)
HOPS = [(j, k) for j in range(4) for k in range(4) if (j, k) != (0, 0)]


class Place:
    def __init__(self):
        self.me = lax.axis_index("rows")
        self.core = lax.rem(self.me, 2)
        self.partner = self.me + 1 - 2 * self.core
        self.spots = tuple(lax.rem(self.me // step, 4) for step in STEPS)

    def shifted(self, dim, j):
        spot = lax.rem(self.spots[dim] + j, 4)
        return spot, (spot - self.spots[dim]) * STEPS[dim]


def remote(src, dst, send, recv, device):
    return pltpu.make_async_remote_copy(src_ref=src, dst_ref=dst, send_sem=send, recv_sem=recv, device_id={"rows": device}, device_id_type=pl.DeviceIdType.MESH)


def greet(place):
    barrier = pltpu.get_barrier_semaphore()
    peers = [place.partner]
    for dim in range(3):
        for j in range(1, 4):
            peers.append(place.me + place.shifted(dim, j)[1])
            peers += [place.me + place.shifted(dim, j)[1] + place.shifted((dim + 1) % 3, k)[1] for k in range(1, 4)]
    for peer in peers:
        pl.semaphore_signal(barrier, inc=1, device_id={"rows": peer}, device_id_type=pl.DeviceIdType.MESH)
    return lambda: pl.semaphore_wait(barrier, len(peers))


def sum_scratch():
    return [
        pltpu.VMEM((3, 3, FIRST, TILE), F32),
        pltpu.VMEM((3, PLANE, TILE), F32),
        pltpu.VMEM((3, 15, PIECE, TILE), F32),
        pltpu.VMEM((3, PLANE, TILE), F32),
        pltpu.VMEM((PADDED, TILE), F32),
        pltpu.SemaphoreType.DMA((2, 108)),
    ]


def span(start, size):
    return pl.ds(pl.multiple_of(start, 8), size)


def all_sum(place, g_ref, got1, acc, got2, full, out, sems, inv_rows, meanwhile):
    copies = []

    def send(src, dst, device):
        copy = remote(src, dst, sems.at[0, len(copies)], sems.at[1, len(copies)], device)
        copy.start()
        copies.append(copy)
        return copy

    def line(t):
        return [(j, *place.shifted(t, j)) for j in (2, 1, 3)]

    def plane(t):
        u, v = (t + 1) % 3, (t + 2) % 3
        for j, k in HOPS:
            (spot1, step1), (spot2, step2) = place.shifted(u, j), place.shifted(v, k)
            yield (spot1 * 4 + spot2) * PIECE, place.me + step1 + step2

    mine = [span(PART * t + place.spots[t] * FIRST, FIRST) for t in range(3)]
    piece = [span((place.spots[(t + 1) % 3] * 4 + place.spots[(t + 2) % 3]) * PIECE, PIECE) for t in range(3)]
    first, second, third, last = [], [], [], []
    for t in range(3):
        first.append([send(g_ref.at[span(PART * t + spot * FIRST, FIRST)], got1.at[t, j - 1], place.me + step) for j, spot, step in line(t)])
    meanwhile()
    for t in range(3):
        acc[t, FIRST:] = jnp.zeros((PLANE - FIRST, TILE), F32)
        for copy in first[t]:
            copy.wait_recv()
        acc[t, 0:FIRST] = (g_ref[mine[t], :] + got1[t, 0]) + (got1[t, 1] + got1[t, 2])
        second.append([send(acc.at[t, span(start, PIECE)], got2.at[t, i], device) for i, (start, device) in enumerate(plane(t))])
    for t in range(3):
        total = acc[t, piece[t]]
        for i, copy in enumerate(second[t]):
            copy.wait_recv()
            total = total + got2[t, i]
        full[t, piece[t]] = total * inv_rows
        spot = full.at[t, piece[t]]
        third.append([send(spot, spot, device) for _, device in plane(t)])
    for t in range(3):
        for copy in third[t]:
            copy.wait_recv()
        last.append([send(full.at[t, 0:FIRST], out.at[mine[t]], place.me + step) for _, _, step in line(t)])
        out[mine[t], :] = full[t, 0:FIRST]
    for t in range(3):
        for copy in last[t]:
            copy.wait_recv()
    for copy in copies:
        copy.wait_send()


def gram_add(x, top, low):
    top[...] = top[...] + dot(x[:, 0:H], x[...], 0, 0)
    low[...] = low[...] + dot(x[:, H:], x[:, H:], 0, 0)


def clear(*refs):
    for ref in refs:
        ref[...] = jnp.zeros_like(ref)


def pack(top, low, dst, extra=None):
    for i, (p, q) in enumerate(BLOCKS):
        src, off = (top, 0) if p < 2 else (low, H)
        x = src[TILE * p - off:TILE * p - off + TILE, TILE * q - off:TILE * q - off + TILE]
        here = slice(TILE * i, TILE * i + TILE)
        dst[here, :] = x if extra is None else x + extra[here, :]
    dst[PACKED:, :] = jnp.zeros((PADDED - PACKED, TILE), F32)


def first_kernel(inv_rows, a_ref, b_ref, out_ref, rows_ref, x, top, low, g, gx, local, swap, *scratch):
    place = Place()
    greeted = greet(place)
    chunks = ROWS // CHUNK

    def fetch(src, dst, half, i):
        return pltpu.make_async_copy(src.at[span(i * CHUNK, CHUNK)], dst.at[span(half * ROWS + i * CHUNK, CHUNK)], local.at[half, i])

    for c, (other, own) in enumerate(((b_ref, a_ref), (a_ref, b_ref))):
        @pl.when(place.core == c)
        def _():
            for i in range(chunks):
                fetch(other, x, 0, i).start()
            for i in range(chunks):
                fetch(own, rows_ref, 1, i).start()

    def add(half, src):
        def body(i, carry):
            fetch(a_ref, src, half, i).wait()
            gram_add(src.at[span(half * ROWS + i * CHUNK, CHUNK)], top, low)
            return carry
        clear(top, low)
        lax.fori_loop(0, chunks, body, 0)

    add(0, x)
    pack(top, low, g.at[0])
    greeted()
    give = remote(g.at[0], gx, swap.at[0], swap.at[1], place.partner)
    give.start()
    add(1, rows_ref)
    give.wait_recv()
    swap_rows = remote(x, rows_ref.at[0:ROWS], swap.at[2], swap.at[3], place.partner)
    pack(top, low, g.at[1], gx)
    *work, out, sems = scratch
    all_sum(place, g.at[1], *work, out, sems, inv_rows, swap_rows.start)
    out_ref[...] = out[0:PACKED, :]
    give.wait_send()
    swap_rows.wait()


def first_sum(a, b, inv_rows):
    return pl.pallas_call(
        functools.partial(first_kernel, inv_rows),
        name="first_sum",
        out_shape=[shape(PACKED, TILE), shape(2 * ROWS, COLS)],
        in_specs=[HBM, HBM],
        out_specs=[VMEM, VMEM],
        scratch_shapes=[
            pltpu.VMEM((ROWS, COLS), F32),
            pltpu.VMEM((H, COLS), F32),
            pltpu.VMEM((H, H), F32),
            pltpu.VMEM((2, PADDED, TILE), F32),
            pltpu.VMEM((PADDED, TILE), F32),
            pltpu.SemaphoreType.DMA((2, ROWS // CHUNK)),
            pltpu.SemaphoreType.DMA((4,)),
            *sum_scratch(),
        ],
        compiler_params=pltpu.CompilerParams(collective_id=0, vmem_limit_bytes=MIB * 52, has_side_effects=True),
    )(a, b)


def solve_into(x, m, dst):
    dst[:, 0:H] = dot(x[:, 0:H], m[0:H, 0:H], 1, 1)
    dst[:, H:] = dot(x[...], m[H:, :], 1, 1)


def second_kernel(inv_rows, rows_ref, m_ref, out_ref, q_ref, q, top, low, g, swap, *scratch):
    place = Place()
    greeted = greet(place)
    swap_rows = remote(q.at[0:ROWS], q_ref.at[0:ROWS], swap.at[0], swap.at[1], place.partner)
    clear(top, low)

    def body(i, carry):
        @pl.when(i == ROWS // CHUNK)
        def _():
            greeted()
            swap_rows.start()
        here = span(i * CHUNK, CHUNK)
        solve_into(rows_ref.at[here], m_ref, q.at[here])
        gram_add(q.at[here], top, low)
        return carry

    lax.fori_loop(0, 2 * ROWS // CHUNK, body, 0)
    pack(top, low, g)

    def keep():
        q_ref[ROWS:, :] = q[ROWS:, :]

    *work, out, sems = scratch
    all_sum(place, g, *work, out, sems, inv_rows, keep)
    out_ref[...] = out[0:PACKED, :]
    swap_rows.wait()


def second_sum(rows, m, inv_rows):
    return pl.pallas_call(
        functools.partial(second_kernel, inv_rows),
        name="second_sum",
        out_shape=[shape(PACKED, TILE), shape(2 * ROWS, COLS)],
        in_specs=[VMEM, VMEM],
        out_specs=[VMEM, VMEM],
        scratch_shapes=[
            pltpu.VMEM((2 * ROWS, COLS), F32),
            pltpu.VMEM((H, COLS), F32),
            pltpu.VMEM((H, H), F32),
            pltpu.VMEM((PADDED, TILE), F32),
            pltpu.SemaphoreType.DMA((2,)),
            *sum_scratch(),
        ],
        compiler_params=pltpu.CompilerParams(collective_id=1, vmem_limit_bytes=MIB * 24, has_side_effects=True),
    )(rows, m)


def share_kernel(m_ref, r_ref, m_out, r_out, sems):
    place = Place()
    barrier = pltpu.get_barrier_semaphore()
    pl.semaphore_signal(barrier, inc=1, device_id={"rows": place.partner}, device_id_type=pl.DeviceIdType.MESH)
    pl.semaphore_wait(barrier, 1)
    lo, hi, every = pl.ds(0, H), pl.ds(H, H), pl.ds(0, COLS)
    moves = [(m_ref, m_out, hi, every), (m_ref, m_out, lo, lo), (r_ref, r_out, lo, every), (r_ref, r_out, hi, hi)]
    copies = []
    for i, (src, dst, rows, cols) in enumerate(moves):
        copies.append(remote(src.at[rows, cols], dst.at[rows, cols], sems.at[0, i], sems.at[1, i], place.partner))
        copies[-1].start()
    m_out[lo, hi] = jnp.zeros((H, H), F32)
    r_out[hi, lo] = jnp.zeros((H, H), F32)
    for copy in copies:
        copy.wait()


def share(m, r):
    return pl.pallas_call(
        share_kernel,
        name="share",
        out_shape=[shape(COLS, COLS)] * 2,
        in_specs=[VMEM] * 2,
        out_specs=[VMEM] * 2,
        scratch_shapes=[pltpu.SemaphoreType.DMA((2, 4))],
        compiler_params=pltpu.CompilerParams(collective_id=2, vmem_limit_bytes=MIB * 8, has_side_effects=True),
    )(m, r)


def last_kernel(other_ref, own_ref, m_other, m_own, r_other, r_own, qa_ref, qb_ref, ra_ref, rb_ref):
    core = lax.rem(lax.axis_index("rows"), 2)
    for c, (q_own, q_other, ro, rp) in enumerate(((qa_ref, qb_ref, ra_ref, rb_ref), (qb_ref, qa_ref, rb_ref, ra_ref))):
        @pl.when(core == c)
        def _():
            solve_into(own_ref, m_own, q_own)
            solve_into(other_ref, m_other, q_other)
            ro[...] = r_own[...]
            rp[...] = r_other[...]


def last_solve(q, m_own, r_own, m_other, r_other):
    steps = 4
    rows = pl.BlockSpec((ROWS // steps, COLS), lambda i: (i, 0))
    more = pl.BlockSpec((ROWS // steps, COLS), lambda i: (i + steps, 0))
    tri = pl.BlockSpec((COLS // steps, COLS), lambda i: (i, 0))
    return pl.pallas_call(
        last_kernel,
        name="last_solve",
        grid=(steps,),
        out_shape=[shape(ROWS, COLS)] * 2 + [shape(COLS, COLS)] * 2,
        in_specs=[rows, more, VMEM, VMEM, tri, tri],
        out_specs=[rows, rows, tri, tri],
        compiler_params=pltpu.CompilerParams(vmem_limit_bytes=MIB * 16),
    )(q, q, m_other, m_own, r_other, r_own)


def solution(mesh):
    row_spec = P(("batch", "rows"), None)
    tri_spec = P("batch", None)
    inv_rows = 1.0 / (ROWS * mesh.shape["rows"])

    def local_qr(a, b):
        gram1, rows = first_sum(a, b, inv_rows)
        u1, m1 = chol(gram1)
        gram2, q = second_sum(rows, m1, inv_rows)
        m2, r = refine(gram2, u1)
        qa, qb, ra, rb = last_solve(q, m2, r, *share(m2, r))
        return qa, ra, qb, rb

    return jax.shard_map(local_qr, mesh=mesh, in_specs=(row_spec, row_spec), out_specs=(row_spec, tri_spec, row_spec, tri_spec), check_vma=False)
```

time: 146 us -> 107 us (0.73)
  Pallas kernels: 142 us -> 106 us
  local copies, waits for them, and re-layouts: 2.57 us -> 0.01 us
    pallas_call x3, Pallas kernels: 49.8 us -> 31.3 us  [the longest x1 17.7 us: chol(): pl.pallas_call(factor_all, name='chol', out_shape=[shape(COLS, COLS)] * 2...]
    pallas_call x1, Pallas kernels: 41.3 us -> 31 us  [second_sum(): pl.pallas_call(functools.partial(second_kernel, inv_rows), name='second_s...]
    pallas_call x1, Pallas kernels: 14.6 us -> 8.71 us  [share(): pl.pallas_call(share_kernel, name='share', out_shape=[shape(COLS, COLS)]...]
    unnamed x6 -> x2, local copies, waits for them, and re-layouts: 2.57 us -> 0.01 us
    pallas_call x1, Pallas kernels: 36.7 us -> 34.8 us  [first_sum(): pl.pallas_call(functools.partial(first_kernel, inv_rows), name='first_sum...]
where the time goes in v2:
time: 107 us; the launch traced here: 106 us
  Pallas kernels  106 us (99%)
    pallas_call x1, Pallas kernels, first_sum(): pl.pallas_call(functools.partial(first_kernel, inv_rows), name='first_sum...  34.8 us
    pallas_call x1, Pallas kernels, second_sum(): pl.pallas_call(functools.partial(second_kernel, inv_rows), name='second_s...  31 us
    pallas_call x1, Pallas kernels, chol(): pl.pallas_call(factor_all, name='chol', out_shape=[shape(COLS, COLS)] * 2...  17.7 us
    pallas_call x1, Pallas kernels, share(): pl.pallas_call(share_kernel, name='share', out_shape=[shape(COLS, COLS)]...  8.71 us
    pallas_call x1, Pallas kernels, last_solve(): pl.pallas_call(last_kernel, name='last_solve', grid=(steps,), out_shape=[...  7.69 us
    pallas_call x1, Pallas kernels, refine(): pl.pallas_call(refine_kernel, name='refine', out_shape=[shape(COLS, COLS)...  5.9 us

profile of v2, /device:TPU:1, one launch (start us, length us, event | category | flops | bytes accessed | tf_op | source)
XLA Modules:
  0.0 106.4 jit_solution(16896743504389726673)
XLA Ops:
  0.6 34.8 %first_sum.1 = (f32[1280,128]{1,0:T(8,128)S(1)}, f32[2048,512]{1,0:T(8,128)}) custom-call(f32[1024,512]{1,0:T(8,128)} %a_ref.1, f32[1024,512]{1,0:T(8,128)} %b_ref.1), custom_call_target="tpu_custom_call" | custom-call | tf_op jit(solution)/shard_map/first_sum/pallas_call | solution.py:375
  35.4 0.0 copy-start
  35.4 17.7 %chol.1 = (f32[512,512]{1,0:T(8,128)S(1)}, f32[512,512]{1,0:T(8,128)S(1)}) custom-call(f32[1280,128]{1,0:T(8,128)S(1)} %get-tuple-element.19.g_ref), custom_call_target="tpu_custom_call" | custom-call | flops 10000000000 | bytes 3145728 | tf_op jit(solution)/shard_map/chol/pallas_call | solution.py:120
  53.1 0.0 copy-done
  53.1 31.0 %second_sum.1 = (f32[1280,128]{1,0:T(8,128)S(1)}, f32[2048,512]{1,0:T(8,128)S(1)}) custom-call(f32[2048,512]{1,0:T(8,128)S(1)} %copy-done, f32[512,512]{1,0:T(8,128)S(1)} %get-tuple-element.20.m_ref), custom_call_target="tpu_custom_call" | custom-call | tf_op jit(solution)/shard_map/second_sum/pallas_call | solution.py:429
  84.1 5.9 %refine.1 = (f32[512,512]{1,0:T(8,128)S(1)}, f32[512,512]{1,0:T(8,128)S(1)}) custom-call(f32[1280,128]{1,0:T(8,128)S(1)} %get-tuple-element.22.g_ref, f32[512,512]{1,0:T(8,128)S(1)} %get-tuple-element.23.u1_ref), custom_call_target="tpu_custom_call" | custom-call | tf_op jit(solution)/shard_map/refine/pallas_call | solution.py:207
  90.0 8.7 %share.1 = (f32[512,512]{1,0:T(8,128)S(1)}, f32[512,512]{1,0:T(8,128)S(1)}) custom-call(f32[512,512]{1,0:T(8,128)S(1)} %get-tuple-element.24.m_ref.m_own, f32[512,512]{1,0:T(8,128)S(1)} %get-tuple-element.25.r_ref.r_own), custom_call_target="tpu_custom_call" | custom-call | tf_op jit(solution)/shard_map/share/pallas_call | solution.py:465
  98.7 7.7 %last_solve.1 = (f32[1024,512]{1,0:T(8,128)}, f32[1024,512]{1,0:T(8,128)}, f32[512,512]{1,0:T(8,128)}, f32[512,512]{1,0:T(8,128)}) custom-call(f32[2048,512]{1,0:T(8,128)S(1)} %get-tuple-element.21.other_ref.own_ref, f32[2048,512]{1,0:T(8,128)S(1)} %get-tuple-element.21.other_ref.own_ref, f32[512,512]{1,0:T(8,128)S(1)} %get-tuple-element.26.m_other, ...), custom_call_target="tpu_custom_call" | custom-call | tf_op jit(solution)/shard_map/last_solve/pallas_call | solution.py:492
Async XLA Ops:
  35.4 17.7 %copy-start = (f32[2048,512]{1,0:T(8,128)S(1)}, f32[2048,512]{1,0:T(8,128)}, u32[]{:S(2)}) copy-start(f32[2048,512]{1,0:T(8,128)} %get-tuple-element.18.rows_ref) | copy-start | bytes 12582916

commit v3 on v2

--- a/solution.py
+++ b/solution.py
@@ -17,9 +17,10 @@
 FIRST = 112
 PART = 4 * FIRST
 PADDED = 3 * PART
-PIECE = 8
-PLANE = 16 * PIECE
+PIECE = 32
+PLANE = 4 * PIECE
 CHUNK = 512
+NEAR = 3
 H = COLS // 2
 MIB = 1 << 20
 VMEM = pl.BlockSpec(memory_space=pltpu.VMEM)
@@ -45,39 +46,65 @@
 def factor_block(d_ref, w_ref):
     sub = lax.broadcasted_iota(jnp.int32, (8, TILE), 0)
     lane = lax.broadcasted_iota(jnp.int32, (8, TILE), 1)
-    for kb in range(16):
+    tiles = TILE // 8
+    at = [slice(8 * m, 8 * m + 8) for m in range(tiles)]
+    cols = [col_of(d_ref[at[0], :], j) for j in range(8)]
+    for kb in range(tiles):
         lo = 8 * kb
-        rows = d_ref[lo:lo + 8, :]
-        inv = w_ref[lo:lo + 8, :] + jnp.where(lane == sub + lo, 1.0, 0.0)
-        cols = [col_of(rows, lo + j) for j in range(8)]
-        scale, urow, wrow, low = [], [], [], {}
+        held = d_ref[at[kb], :]
+        rows = held
+        inv = jnp.where(lane < lo, held, jnp.where(lane == sub + lo, 1.0, 0.0))
+        done = lane < lo + 8
+        here = (lane >= lo) & done
+        ahead = kb + 1 < tiles
+        if ahead:
+            nxt = d_ref[at[kb + 1], :]
+            side = [col_of(nxt, lo + j) for j in range(8)]
+            coming = [col_of(nxt, lo + 8 + j) for j in range(8)]
+            nxt = jnp.where(here, 0.0, nxt)
+        low, both = {}, []
+        scale = jnp.zeros((8, TILE), F32)
         for k in range(8):
             rs = lax.rsqrt(row_of(cols[k], k))
-            lk = cols[k] * rs
+            ri = rs * rs
             for j in range(k + 1, 8):
-                low[j, k] = row_of(lk, j)
-                cols[j] = cols[j] - lk * low[j, k]
-            u, w = row_of(rows, k) * rs, row_of(inv, k) * rs
-            lm = jnp.where(sub > k, lk, 0.0)
-            rows = jnp.where(sub == k, u, rows - lm * u)
-            inv = jnp.where(sub == k, w, inv - lm * w)
-            scale.append(rs)
-            urow.append(u)
-            wrow.append(w)
-        d_ref[lo:lo + 8, :] = jnp.where(lane >= sub + lo, rows, 0.0)
-        w_ref[lo:lo + 8, :] = inv
-        for m in range(kb + 1, 16):
-            r = d_ref[8 * m:8 * m + 8, :]
-            v = w_ref[8 * m:8 * m + 8, :]
-            cs = [col_of(r, lo + j) for j in range(8)]
+                low[j, k] = row_of(cols[k], j) * ri
+                cols[j] = cols[j] - cols[k] * low[j, k]
+            if ahead:
+                part = side[k] * ri
+                for j in range(k + 1, 8):
+                    side[j] = side[j] - side[k] * low[j, k]
+                for j in range(8):
+                    coming[j] = coming[j] - side[k] * row_of(part, j)
+            u, w = row_of(rows, k) * ri, row_of(inv, k) * ri
+            below = jnp.where(sub > k, cols[k], 0.0)
+            rows = rows - below * u
+            inv = inv - below * w
+            scale = jnp.where(sub == k, rs, scale)
+            both.append(jnp.where(done, w, u))
+            if ahead:
+                nxt = nxt - side[k] * both[k]
+        d_ref[at[kb], :] = jnp.where(lane >= sub + lo, rows * scale, 0.0)
+        w_ref[at[kb], :] = inv * scale
+        if ahead:
+            d_ref[at[kb + 1], :] = nxt
+            cols = coming
+        for m in range(kb + 2, tiles if kb >= tiles // 2 else tiles // 2 + NEAR):
+            x = d_ref[at[m], :]
+            side = [col_of(x, lo + j) for j in range(8)]
+            x = jnp.where(here, 0.0, x)
             for k in range(8):
-                lk = cs[k] * scale[k]
                 for j in range(k + 1, 8):
-                    cs[j] = cs[j] - lk * low[j, k]
-                r = r - lk * urow[k]
-                v = v - lk * wrow[k]
-            d_ref[8 * m:8 * m + 8, :] = r
-            w_ref[8 * m:8 * m + 8, :] = v
+                    side[j] = side[j] - side[k] * low[j, k]
+                x = x - side[k] * both[k]
+            d_ref[at[m], :] = x
+        if kb == tiles // 2 - 1:
+            half = TILE // 2
+            upper = d_ref[0:half, :]
+            wide = lax.broadcasted_iota(jnp.int32, (half, TILE), 1)
+            band = dot(upper, jnp.where(wide < half, w_ref[0:half, :], upper), 0, 0)
+            for m in range(tiles // 2 + NEAR, tiles):
+                d_ref[at[m], :] = jnp.where(lane < half, 0.0, d_ref[at[m], :]) - band[at[m], :]
 
 
 def factor_all(g_ref, u_ref, m_ref, s_ref, d_ref, w_ref):
@@ -87,7 +114,6 @@
     d_ref[...] = g_ref[0:TILE, :]
 
     def panel(p, carry):
-        w_ref[...] = jnp.zeros_like(w_ref)
         factor_block(d_ref, w_ref)
         for pp in range(4):
             @pl.when(p == pp)
@@ -216,7 +242,6 @@
 
 
 STEPS = (2, 8, 32)
-HOPS = [(j, k) for j in range(4) for k in range(4) if (j, k) != (0, 0)]
 
 
 class Place:
@@ -237,11 +262,7 @@
 
 def greet(place):
     barrier = pltpu.get_barrier_semaphore()
-    peers = [place.partner]
-    for dim in range(3):
-        for j in range(1, 4):
-            peers.append(place.me + place.shifted(dim, j)[1])
-            peers += [place.me + place.shifted(dim, j)[1] + place.shifted((dim + 1) % 3, k)[1] for k in range(1, 4)]
+    peers = [place.partner] + [place.me + place.shifted(dim, j)[1] for dim in range(3) for j in range(1, 4)]
     for peer in peers:
         pl.semaphore_signal(barrier, inc=1, device_id={"rows": peer}, device_id_type=pl.DeviceIdType.MESH)
     return lambda: pl.semaphore_wait(barrier, len(peers))
@@ -251,10 +272,11 @@
     return [
         pltpu.VMEM((3, 3, FIRST, TILE), F32),
         pltpu.VMEM((3, PLANE, TILE), F32),
-        pltpu.VMEM((3, 15, PIECE, TILE), F32),
+        pltpu.VMEM((3, 3, PIECE, TILE), F32),
+        pltpu.VMEM((3, 4, PIECE, TILE), F32),
         pltpu.VMEM((3, PLANE, TILE), F32),
         pltpu.VMEM((PADDED, TILE), F32),
-        pltpu.SemaphoreType.DMA((2, 108)),
+        pltpu.SemaphoreType.DMA((2, 45)),
     ]
 
 
@@ -262,7 +284,7 @@
     return pl.ds(pl.multiple_of(start, 8), size)
 
 
-def all_sum(place, g_ref, got1, acc, got2, full, out, sems, inv_rows, meanwhile):
+def all_sum(place, g_ref, got1, acc, got2, terms, full, out, sems, inv_rows, meanwhile):
     copies = []
 
     def send(src, dst, device):
@@ -271,42 +293,42 @@
         copies.append(copy)
         return copy
 
-    def line(t):
-        return [(j, *place.shifted(t, j)) for j in (2, 1, 3)]
-
-    def plane(t):
-        u, v = (t + 1) % 3, (t + 2) % 3
-        for j, k in HOPS:
-            (spot1, step1), (spot2, step2) = place.shifted(u, j), place.shifted(v, k)
-            yield (spot1 * 4 + spot2) * PIECE, place.me + step1 + step2
-
-    mine = [span(PART * t + place.spots[t] * FIRST, FIRST) for t in range(3)]
-    piece = [span((place.spots[(t + 1) % 3] * 4 + place.spots[(t + 2) % 3]) * PIECE, PIECE) for t in range(3)]
-    first, second, third, last = [], [], [], []
+    def line(dim):
+        return [(j, *place.shifted(dim, j)) for j in (2, 1, 3)]
+
+    me, spots = place.me, place.spots
+    mine = [span(PART * t + spots[t] * FIRST, FIRST) for t in range(3)]
+    piece = [span(spots[(t + 1) % 3] * PIECE, PIECE) for t in range(3)]
+    hops = [[] for _ in range(5)]
     for t in range(3):
-        first.append([send(g_ref.at[span(PART * t + spot * FIRST, FIRST)], got1.at[t, j - 1], place.me + step) for j, spot, step in line(t)])
+        hops[0].append([send(g_ref.at[span(PART * t + spot * FIRST, FIRST)], got1.at[t, j - 1], me + step) for j, spot, step in line(t)])
     meanwhile()
     for t in range(3):
         acc[t, FIRST:] = jnp.zeros((PLANE - FIRST, TILE), F32)
-        for copy in first[t]:
+        for copy in hops[0][t]:
             copy.wait_recv()
         acc[t, 0:FIRST] = (g_ref[mine[t], :] + got1[t, 0]) + (got1[t, 1] + got1[t, 2])
-        second.append([send(acc.at[t, span(start, PIECE)], got2.at[t, i], device) for i, (start, device) in enumerate(plane(t))])
+        hops[1].append([send(acc.at[t, span(spot * PIECE, PIECE)], got2.at[t, j - 1], me + step) for j, spot, step in line((t + 1) % 3)])
     for t in range(3):
-        total = acc[t, piece[t]]
-        for i, copy in enumerate(second[t]):
+        third = (t + 2) % 3
+        for copy in hops[1][t]:
             copy.wait_recv()
-            total = total + got2[t, i]
-        full[t, piece[t]] = total * inv_rows
-        spot = full.at[t, piece[t]]
-        third.append([send(spot, spot, device) for _, device in plane(t)])
+        terms[t, spots[third]] = (acc[t, piece[t]] + got2[t, 0]) + (got2[t, 1] + got2[t, 2])
+        term = terms.at[t, spots[third]]
+        hops[2].append([send(term, term, me + step) for _, _, step in line(third)])
     for t in range(3):
-        for copy in third[t]:
+        for copy in hops[2][t]:
             copy.wait_recv()
-        last.append([send(full.at[t, 0:FIRST], out.at[mine[t]], place.me + step) for _, _, step in line(t)])
+        full[t, piece[t]] = ((terms[t, 0] + terms[t, 1]) + (terms[t, 2] + terms[t, 3])) * inv_rows
+        here = full.at[t, piece[t]]
+        hops[3].append([send(here, here, me + step) for _, _, step in line((t + 1) % 3)])
+    for t in range(3):
+        for copy in hops[3][t]:
+            copy.wait_recv()
+        hops[4].append([send(full.at[t, 0:FIRST], out.at[mine[t]], me + step) for _, _, step in line(t)])
         out[mine[t], :] = full[t, 0:FIRST]
-    for t in range(3):
-        for copy in last[t]:
+    for group in hops[4]:
+        for copy in group:
             copy.wait_recv()
     for copy in copies:
         copy.wait_send()

time: 107 us -> 99.9 us (0.934)
  Pallas kernels: 106 us -> 99.1 us
    pallas_call x1, Pallas kernels: 17.7 us -> 12.9 us  [chol(): pl.pallas_call(factor_all, name='chol', out_shape=[shape(COLS, COLS)] * 2...]
    pallas_call x1, Pallas kernels: 31 us -> 28.1 us  [second_sum(): pl.pallas_call(functools.partial(second_kernel, inv_rows), name='second_s...]
    pallas_call x1, Pallas kernels: 8.71 us -> 11.5 us  [share(): pl.pallas_call(share_kernel, name='share', out_shape=[shape(COLS, COLS)]...]
    pallas_call x1, Pallas kernels: 34.8 us -> 32.9 us  [first_sum(): pl.pallas_call(functools.partial(first_kernel, inv_rows), name='first_sum...]
where the time goes in v3:
time: 99.9 us; the launch traced here: 99.8 us
  Pallas kernels  99.1 us (99%)
    pallas_call x1, Pallas kernels, first_sum(): pl.pallas_call(functools.partial(first_kernel, inv_rows), name='first_sum...  32.9 us
    pallas_call x1, Pallas kernels, second_sum(): pl.pallas_call(functools.partial(second_kernel, inv_rows), name='second_s...  28.1 us
    pallas_call x1, Pallas kernels, chol(): pl.pallas_call(factor_all, name='chol', out_shape=[shape(COLS, COLS)] * 2...  12.9 us
    pallas_call x1, Pallas kernels, share(): pl.pallas_call(share_kernel, name='share', out_shape=[shape(COLS, COLS)]...  11.5 us
    pallas_call x1, Pallas kernels, last_solve(): pl.pallas_call(last_kernel, name='last_solve', grid=(steps,), out_shape=[...  7.69 us
    pallas_call x1, Pallas kernels, refine(): pl.pallas_call(refine_kernel, name='refine', out_shape=[shape(COLS, COLS)...  5.9 us

profile of v3, /device:TPU:1, one launch (start us, length us, event | category | flops | bytes accessed | tf_op | source)
XLA Modules:
  0.0 99.8 jit_solution(11569007548203861955)
XLA Ops:
  0.6 32.9 %first_sum.1 = (f32[1280,128]{1,0:T(8,128)S(1)}, f32[2048,512]{1,0:T(8,128)}) custom-call(f32[1024,512]{1,0:T(8,128)} %a_ref.1, f32[1024,512]{1,0:T(8,128)} %b_ref.1), custom_call_target="tpu_custom_call" | custom-call | tf_op jit(solution)/shard_map/first_sum/pallas_call | solution.py:397
  33.6 0.0 copy-start
  33.6 12.9 %chol.1 = (f32[512,512]{1,0:T(8,128)S(1)}, f32[512,512]{1,0:T(8,128)S(1)}) custom-call(f32[1280,128]{1,0:T(8,128)S(1)} %get-tuple-element.19.g_ref), custom_call_target="tpu_custom_call" | custom-call | flops 10000000000 | bytes 3145728 | tf_op jit(solution)/shard_map/chol/pallas_call | solution.py:146
  46.5 0.0 copy-done
  46.5 28.1 %second_sum.1 = (f32[1280,128]{1,0:T(8,128)S(1)}, f32[2048,512]{1,0:T(8,128)S(1)}) custom-call(f32[2048,512]{1,0:T(8,128)S(1)} %copy-done, f32[512,512]{1,0:T(8,128)S(1)} %get-tuple-element.20.m_ref), custom_call_target="tpu_custom_call" | custom-call | tf_op jit(solution)/shard_map/second_sum/pallas_call | solution.py:451
  74.7 5.9 %refine.1 = (f32[512,512]{1,0:T(8,128)S(1)}, f32[512,512]{1,0:T(8,128)S(1)}) custom-call(f32[1280,128]{1,0:T(8,128)S(1)} %get-tuple-element.22.g_ref, f32[512,512]{1,0:T(8,128)S(1)} %get-tuple-element.23.u1_ref), custom_call_target="tpu_custom_call" | custom-call | tf_op jit(solution)/shard_map/refine/pallas_call | solution.py:233
  80.6 11.5 %share.1 = (f32[512,512]{1,0:T(8,128)S(1)}, f32[512,512]{1,0:T(8,128)S(1)}) custom-call(f32[512,512]{1,0:T(8,128)S(1)} %get-tuple-element.24.m_ref.m_own, f32[512,512]{1,0:T(8,128)S(1)} %get-tuple-element.25.r_ref.r_own), custom_call_target="tpu_custom_call" | custom-call | tf_op jit(solution)/shard_map/share/pallas_call | solution.py:487
  92.1 7.7 %last_solve.1 = (f32[1024,512]{1,0:T(8,128)}, f32[1024,512]{1,0:T(8,128)}, f32[512,512]{1,0:T(8,128)}, f32[512,512]{1,0:T(8,128)}) custom-call(f32[2048,512]{1,0:T(8,128)S(1)} %get-tuple-element.21.other_ref.own_ref, f32[2048,512]{1,0:T(8,128)S(1)} %get-tuple-element.21.other_ref.own_ref, f32[512,512]{1,0:T(8,128)S(1)} %get-tuple-element.26.m_other, ...), custom_call_target="tpu_custom_call" | custom-call | tf_op jit(solution)/shard_map/last_solve/pallas_call | solution.py:514
Async XLA Ops:
  33.6 13.0 %copy-start = (f32[2048,512]{1,0:T(8,128)S(1)}, f32[2048,512]{1,0:T(8,128)}, u32[]{:S(2)}) copy-start(f32[2048,512]{1,0:T(8,128)} %get-tuple-element.18.rows_ref) | copy-start | bytes 12582916
